TPU v7x, 128 devices: a whole 4x4x4 slice. The times are simulated.
128 devices in a mesh: rows: 8 (over y_hi, z), bundle: 16 (over y_lo, x, core).
Axes of the slice: x: 4, y: 4 (y_hi: 2, y_lo: 2; y = y_hi * 2 + y_lo), z: 4, core: 2. Of those that a mesh axis runs over, the one named last changes fastest.
Arguments:
- raw_values: float32 [32768, 4096], P(('rows', 'bundle')), may hold values from -2100 to 2100
- bin_edges: float32 [4096, 255], P(('rows', 'bundle')), may hold values from -2100 to 2100, as said below
- feature_column: int32 [4096], replicated, may hold values from 0 to 4095, each once
- bin_offset: int32 [4096], replicated, may hold values from 0 to 63
Outputs:
- bin_codes: int32 [32768, 4096], P('rows', 'bundle')
Inputs may be any that keep to these rules, and one draw needn't show every extreme that they name: Every row of bin_edges is strictly increasing. `feature_column`: each column 0 .. 4095 is named once.
All inputs are finite; a program needn't handle non-finite values.
Results may differ from a plain program's by a relative error of at most 0.0003.
Values may be sent and summed in bfloat16 or wider, within the bound.
No kernel may reach another device: no remote copies, remote signals or barrier semaphores. Data moves between devices by JAX's collectives and lax.ppermute only.
A program may use at most 64 MiB of HBM per device.

v0:
```python
import math

import jax
import jax.numpy as jnp
from jax import lax
from jax.sharding import PartitionSpec as P


def count_below(values, edges):
    total = values.shape[0]
    block = math.gcd(total, 512)

    def one_block(part_rows):
        return jnp.sum(part_rows[:, :, None] > edges[None, :, :], axis=2, dtype=jnp.int32)

    blocks = values.reshape(total // block, block, values.shape[1])
    return lax.map(one_block, blocks).reshape(total, values.shape[1])


def local(raw_values, bin_edges, feature_column, bin_offset):
    count_feat = feature_column.shape[0]
    owner_feature = (
        jnp.zeros((count_feat,), jnp.int32)
        .at[feature_column]
        .set(jnp.arange(count_feat, dtype=jnp.int32))
    )
    edges_all = lax.all_gather(bin_edges, ("rows", "bundle"), axis=0, tiled=True)
    span_cols = count_feat // lax.axis_size("bundle")
    first_col = lax.axis_index("bundle") * span_cols
    owned_features = lax.dynamic_slice_in_dim(owner_feature, first_col, span_cols, 0)
    owned_offsets = jnp.take(bin_offset, owned_features)
    ordered = jnp.take(raw_values, owner_feature, axis=1)
    arrived = lax.all_to_all(ordered, "bundle", split_axis=1, concat_axis=0, tiled=True)
    owned_edges = jnp.take(edges_all, owned_features, axis=0)
    bins = count_below(arrived, owned_edges)
    return bins + owned_offsets[None, :]


def solution(mesh):
    in_specs = (P(("rows", "bundle"), None), P(("rows", "bundle"), None), P(), P())
    out_specs = P("rows", "bundle")
    return jax.shard_map(local, mesh=mesh, in_specs=in_specs, out_specs=out_specs, check_vma=False)
```

profile of v0, /device:TPU:1, one launch (start us, length us, event | category | flops | bytes accessed | tf_op | source)
XLA Modules:
  0.0 402.5 jit_solution(2743902135054900471)
XLA Ops:
  7.3 5.6 %copy.9 = f32[256,4096]{0,1:T(8,128)} copy(f32[256,4096]{1,0:T(8,128)} %param.6) | data formatting | bytes 8388608 | tf_op args[0]
  12.9 15.5 %scatter_custom_fusion = s32[4096]{0:T(1024)S(1)} fusion(s32[4096]{0:T(1024)S(1)} %compare_select_fusion.1, s32[4096]{0:T(1024)S(1)} %iota.3, s32[]{:T(128)} %copy.20), kind=kCustom, calls=%fused_computation.14 | custom fusion | bytes 16388 | tf_op jit(solution)/shard_map/scatter | solution.py:25
  28.5 18.4 %gather_fusion = f32[4096,256]{1,0:T(8,128)} fusion(f32[256,4096]{0,1:T(8,128)} %copy.9, s32[4096]{0:T(1024)S(1)} %fusion), kind=kCustom, calls=%fused_computation | custom fusion | bytes 8404992 | tf_op jit(solution)/shard_map/jit(_take)/gather | solution.py:32
  46.9 3.9 broadcast_select_fusion
  50.8 6.8 %all-to-all-start = ((f32[256,16,256]{0,2,1:T(8,128)}), f32[256,16,256]{0,2,1:T(8,128)}, u32[]{:S(2)}, u32[]{:S(2)}) async-start(f32[256,16,256]{0,2,1:T(8,128)} %broadcast_select_fusion), calls=%async_computation | async-start | bytes 8388608 | tf_op jit(solution)/shard_map/all_to_all | solution.py:33
  57.7 1.7 gather_fusion.2
  59.5 55.1 %all-to-all-done = f32[256,16,256]{0,2,1:T(8,128)} async-done(((f32[256,16,256]{0,2,1:T(8,128)}), f32[256,16,256]{0,2,1:T(8,128)}, u32[]{:S(2)}, u32[]{:S(2)}) %all-to-all-start) | async-done | bytes 4194336 | tf_op jit(solution)/shard_map/all_to_all | solution.py:33
  114.6 5.3 %copy.10 = f32[16,256,256]{2,1,0:T(8,128)} copy(f32[16,256,256]{1,2,0:T(8,128)} %bitcast.4) | data formatting | bytes 8388608 | tf_op jit(solution)/shard_map/all_to_all | solution.py:33
  119.9 122.6 %all-gather.2.cloned.1.call-done = f32[4096,255]{1,0:T(8,128)} async-done(((f32[32,255]{1,0:T(8,128)}), f32[4096,255]{1,0:T(8,128)}) %all-gather.2.cloned.1.call-update) | async-done | bytes 4177936 | tf_op jit(solution)/shard_map/all_gather | solution.py:27
  242.6 3.2 gather_fusion.1
  246.0 145.3 %while.10 = (s32[]{:T(128)}, s32[8,512,256]{2,1,0:T(8,128)}, f32[8,512,256]{2,1,0:T(8,128)}, f32[256,255]{0,1:T(8,128)S(1)}, s32[]{:T(128)}) while((s32[]{:T(128)}, s32[8,512,256]{2,1,0:T(8,128)}, f32[8,512,256]{2,1,0:T(8,128)}, f32[256,255]{0,1:T(8,128)S(1)}, s32[]{:T(128)}) %tuple.25), condition=%wide.region_3.4_spmd, body=%wide.region_1.0_spmd.sunk | while | flops 100139008 | bytes 3407425 | solution.py:17
  246.0 1.1 dynamic-slice_bitcast_fusion.2
  247.1 16.2 %convert_reduce_fusion.2 = s32[512,256]{1,0:T(8,128)S(1)} fusion(f32[256,255]{0,1:T(8,128)S(1)} %get-tuple-element.80, f32[512,256]{1,0:T(8,128)S(1)} %dynamic-slice_bitcast_fusion.2), kind=kLoop, calls=%fused_computation.4.clone.1 | loop fusion | flops 100139008 | bytes 1309696 | tf_op jit(solution)/shard_map/while/body/eval_jaxpr/reduce_sum | solution.py:14
  263.3 0.9 bitcast_dynamic-update-slice_fusion.2
  264.1 1.1 dynamic-slice_bitcast_fusion.2
  265.2 16.2 %convert_reduce_fusion.2 = s32[512,256]{1,0:T(8,128)S(1)} fusion(f32[256,255]{0,1:T(8,128)S(1)} %get-tuple-element.80, f32[512,256]{1,0:T(8,128)S(1)} %dynamic-slice_bitcast_fusion.2), kind=kLoop, calls=%fused_computation.4.clone.1 | loop fusion | flops 100139008 | bytes 1309696 | tf_op jit(solution)/shard_map/while/body/eval_jaxpr/reduce_sum | solution.py:14
  282.3 1.1 dynamic-slice_bitcast_fusion.2
  283.4 16.2 %convert_reduce_fusion.2 = s32[512,256]{1,0:T(8,128)S(1)} fusion(f32[256,255]{0,1:T(8,128)S(1)} %get-tuple-element.80, f32[512,256]{1,0:T(8,128)S(1)} %dynamic-slice_bitcast_fusion.2), kind=kLoop, calls=%fused_computation.4.clone.1 | loop fusion | flops 100139008 | bytes 1309696 | tf_op jit(solution)/shard_map/while/body/eval_jaxpr/reduce_sum | solution.py:14
  299.6 0.9 bitcast_dynamic-update-slice_fusion.2
  300.5 1.1 dynamic-slice_bitcast_fusion.2
  301.5 16.2 %convert_reduce_fusion.2 = s32[512,256]{1,0:T(8,128)S(1)} fusion(f32[256,255]{0,1:T(8,128)S(1)} %get-tuple-element.80, f32[512,256]{1,0:T(8,128)S(1)} %dynamic-slice_bitcast_fusion.2), kind=kLoop, calls=%fused_computation.4.clone.1 | loop fusion | flops 100139008 | bytes 1309696 | tf_op jit(solution)/shard_map/while/body/eval_jaxpr/reduce_sum | solution.py:14
  318.6 1.1 dynamic-slice_bitcast_fusion.2
  319.7 16.2 %convert_reduce_fusion.2 = s32[512,256]{1,0:T(8,128)S(1)} fusion(f32[256,255]{0,1:T(8,128)S(1)} %get-tuple-element.80, f32[512,256]{1,0:T(8,128)S(1)} %dynamic-slice_bitcast_fusion.2), kind=kLoop, calls=%fused_computation.4.clone.1 | loop fusion | flops 100139008 | bytes 1309696 | tf_op jit(solution)/shard_map/while/body/eval_jaxpr/reduce_sum | solution.py:14
  335.9 0.9 bitcast_dynamic-update-slice_fusion.2
  336.8 1.1 dynamic-slice_bitcast_fusion.2
  337.8 16.2 %convert_reduce_fusion.2 = s32[512,256]{1,0:T(8,128)S(1)} fusion(f32[256,255]{0,1:T(8,128)S(1)} %get-tuple-element.80, f32[512,256]{1,0:T(8,128)S(1)} %dynamic-slice_bitcast_fusion.2), kind=kLoop, calls=%fused_computation.4.clone.1 | loop fusion | flops 100139008 | bytes 1309696 | tf_op jit(solution)/shard_map/while/body/eval_jaxpr/reduce_sum | solution.py:14
  354.9 1.1 dynamic-slice_bitcast_fusion.2
  356.0 16.2 %convert_reduce_fusion.2 = s32[512,256]{1,0:T(8,128)S(1)} fusion(f32[256,255]{0,1:T(8,128)S(1)} %get-tuple-element.80, f32[512,256]{1,0:T(8,128)S(1)} %dynamic-slice_bitcast_fusion.2), kind=kLoop, calls=%fused_computation.4.clone.1 | loop fusion | flops 100139008 | bytes 1309696 | tf_op jit(solution)/shard_map/while/body/eval_jaxpr/reduce_sum | solution.py:14
  373.0 1.1 dynamic-slice_bitcast_fusion.2
  374.1 16.2 %convert_reduce_fusion.2 = s32[512,256]{1,0:T(8,128)S(1)} fusion(f32[256,255]{0,1:T(8,128)S(1)} %get-tuple-element.80, f32[512,256]{1,0:T(8,128)S(1)} %dynamic-slice_bitcast_fusion.2), kind=kLoop, calls=%fused_computation.4.clone.1 | loop fusion | flops 100139008 | bytes 1309696 | tf_op jit(solution)/shard_map/while/body/eval_jaxpr/reduce_sum | solution.py:14
  390.3 0.9 bitcast_dynamic-update-slice_fusion.2
  391.2 4.5 %bitcast_add_fusion = s32[4096,256]{1,0:T(8,128)} fusion(s32[8,512,256]{2,1,0:T(8,128)} %get-tuple-element.27, s32[256]{0:T(256)S(1)} %get-tuple-element.40), kind=kLoop, calls=%fused_computation.7 | loop fusion | flops 1048576 | bytes 8389632 | tf_op jit(solution)/shard_map/add | solution.py:36
  (21 shorter events, 4.5 us)
Async XLA Ops:
  6.5 51.2 %copy-start = (s32[4096]{0:T(1024)S(1)}, s32[4096]{0:T(1024)}, u32[]{:S(2)}) copy-start(s32[4096]{0:T(1024)} %param.9) | copy-start | bytes 49156
  6.5 236.0 %all-gather.2.cloned.1.call-start = ((), (), s32[]{:S(2)}) async-start(), calls=%async_computation.1 | async-start | bytes 4227072 | tf_op jit(solution)/shard_map/all_gather | solution.py:27
  7.3 5.6 %copy-start.1 = (s32[4096]{0:T(1024)S(1)}, s32[4096]{0:T(1024)}, u32[]{:S(2)}) copy-start(s32[4096]{0:T(1024)} %param.8) | copy-start | bytes 49156
  50.8 63.8 %all-to-all-start = ((f32[256,16,256]{0,2,1:T(8,128)}), f32[256,16,256]{0,2,1:T(8,128)}, u32[]{:S(2)}, u32[]{:S(2)}) async-start(f32[256,16,256]{0,2,1:T(8,128)} %broadcast_select_fusion), calls=%async_computation | async-start | bytes 8388608 | tf_op jit(solution)/shard_map/all_to_all | solution.py:33
Sparse Core Ops, SparseCore 0:
  9.1 233.4 all-gather.1
where the time goes:
time: 403 us
  waiting for transfers between devices  178 us (44%)
  other arithmetic  139 us (34%)
  local copies, waits for them, and re-layouts  65.2 us (16%)
  between operations  13.5 us (3%)
  starting transfers between devices  6.83 us (2%)
    reduce_sum x8, other arithmetic, one_block(): jnp.sum(part_rows[:, :, None] > edges[None, :, :], axis=2, dtype=jnp.int32)  130 us
    all_gather x1, waiting for transfers between devices, local(): lax.all_gather(bin_edges, ('rows', 'bundle'), axis=0, tiled=True)  123 us
    all_to_all x1, waiting for transfers between devices, local(): lax.all_to_all(ordered, 'bundle', split_axis=1, concat_axis=0, tiled=True)  55.1 us
    gather x1, local copies, waits for them, and re-layouts, local(): ordered = jnp.take(raw_values, owner_feature, axis=1)  18.4 us
    scatter x1, local copies, waits for them, and re-layouts, local(): owner_feature = jnp.zeros((count_feat,), jnp.int32).at[feature_column].se...  15.5 us
    gt x8, local copies, waits for them, and re-layouts, one_block(): part_rows[:, :, None] > edges[None, :, :]  8.61 us
  transfers between devices with their start and end apart: 2, of which 2 were waited for; matrix products, arithmetic and copies ran while one was open for 13% of the time, Pallas kernels for 0%

commit v1 on v0

v1 whole, which is shorter than its diff:
```python
import jax
import jax.numpy as jnp
from jax import lax
from jax.experimental import pallas as pl
from jax.experimental.pallas import tpu as pltpu
from jax.sharding import PartitionSpec as P

AXES = ("rows", "bundle")
CHUNKS = 2
WIDE = 4
SIDE = 4


def device_at(y, z, x, core):
    return ((y // 2) * 4 + z) * 16 + (y % 2) * 8 + x * 2 + core


def gather_groups():
    ring = range(SIDE)
    planes = [[device_at(y, z, x, 0) for y in ring for x in ring] for z in ring]
    planes += [[device_at(y, z, x, 1) for z in ring for y in ring] for x in ring]
    lines = [[device_at(y, z, x, 0) for z in ring] for y in ring for x in ring]
    lines += [[device_at(y, z, x, 1) for x in ring] for z in ring for y in ring]
    return planes, lines


def spread(piece, groups):
    copies = jnp.broadcast_to(piece[None], (len(groups[0]), *piece.shape))
    return lax.all_to_all(copies, AXES, split_axis=0, concat_axis=0, axis_index_groups=groups, tiled=True)


def gather_edges(bin_edges):
    planes, lines = gather_groups()
    padded = jnp.pad(bin_edges, ((0, 0), (0, 1)))
    plane = spread(padded, planes)
    mine = spread(plane, lines).reshape(64, 32, 256)
    other = lax.ppermute(mine, "bundle", [(i, i ^ 1) for i in range(16)])
    return mine, other


def pick(table, index):
    dims = lax.GatherDimensionNumbers(
        offset_dims=(),
        collapsed_slice_dims=(0,),
        start_index_map=(0,),
        operand_batching_dims=(1,),
        start_indices_batching_dims=(1,),
    )
    return lax.gather(
        table, index[..., None], dims, (1, 1), mode=lax.GatherScatterMode.PROMISE_IN_BOUNDS
    )


def count_steps(values, table):
    top = table(31)
    group = jnp.where(values > jnp.broadcast_to(top[3:4], values.shape), 4, 0)
    group = jnp.where(values > pick(top, group + 1), group + 2, group)
    group = jnp.where(values > pick(top, group), group + 1, group)

    def at(o):
        return pick(table(o), group)

    b4 = values > at(15)
    b5 = values > jnp.where(b4, at(23), at(7))
    b6 = values > jnp.where(b4, jnp.where(b5, at(27), at(19)), jnp.where(b5, at(11), at(3)))

    def among(o):
        pairs = [jnp.where(b6, at(8 * i + 4 + o), at(8 * i + o)) for i in range(4)]
        return jnp.where(b4, jnp.where(b5, pairs[3], pairs[2]), jnp.where(b5, pairs[1], pairs[0]))

    b7 = values > among(1)
    b8 = values > jnp.where(b7, among(2), among(0))
    count = group * 32
    for bit, weight in ((b4, 16), (b5, 8), (b6, 4), (b7, 2), (b8, 1)):
        count = count + jnp.where(bit, weight, 0)
    return count


def bin_kernel(core_ref, raw_ref, mine_ref, other_ref, column_ref, offset_ref, out_ref, edges, tables, codes, sems):
    core = core_ref[0]
    height = raw_ref.shape[0]
    places = [(y, z, x, side) for y in range(SIDE) for z in range(SIDE) for x in range(SIDE) for side in range(2)]

    def piece(y, z, x, side):
        whose = core if side == 0 else 1 - core
        flat = z * 16 + y * 4 + x
        cross = x * 16 + z * 4 + y
        source = flat + whose * (cross - flat)
        where = device_at(y, z, x, 0) + whose
        ref = mine_ref if side == 0 else other_ref
        return pltpu.make_async_copy(
            ref.at[source], edges.at[pl.ds(where * 32, 32), :], sems.at[device_at(y, z, x, side)]
        )

    for place in places:
        piece(*place).start()
    for place in places:
        piece(*place).wait()

    codes[height:, :] = jnp.zeros((16, codes.shape[1]), codes.dtype)
    codes[height : height + 8, :] = jnp.broadcast_to(
        offset_ref[...].astype(jnp.float32), (8, codes.shape[1])
    ).astype(codes.dtype)

    def one_block(j, carry):
        lanes = pl.ds(pl.multiple_of(j * 128, 128), 128)
        tables[...] = edges[lanes, :].T

        def table(o):
            return tables[pl.ds(o, 8, stride=32), :]

        def some_rows(i, inner):
            parts = []
            for w in range(WIDE):
                rows = pl.ds(pl.multiple_of((i * WIDE + w) * 8, 8), 8)
                parts.append(count_steps(raw_ref[rows, lanes], table))
            whole = jnp.concatenate(parts, axis=0).astype(jnp.float32)
            rows = pl.ds(pl.multiple_of(i * WIDE * 8, WIDE * 8), WIDE * 8)
            codes[rows, lanes] = whole.astype(codes.dtype)
            return inner

        return lax.fori_loop(0, height // (8 * WIDE), some_rows, carry)

    lax.fori_loop(0, codes.shape[1] // 128, one_block, 0)

    span = out_ref.shape[2]

    def one_bundle(d, carry):
        column = column_ref[...] - d * span
        lines = lax.broadcasted_iota(jnp.int32, (span, column.shape[1]), 0)
        chosen = jnp.where(lines == column, 1.0, 0.0).astype(jnp.bfloat16)
        moved = lax.dot_general(
            codes[...], chosen, (((1,), (1,)), ((), ())), preferred_element_type=jnp.float32
        )
        total = moved[:height] + moved[height : height + 1]
        out_ref[d] = total.astype(jnp.int32).astype(jnp.int16)
        return carry

    lax.fori_loop(0, out_ref.shape[0], one_bundle, 0)


def bin_rows(core, raw, part, mine, other, column, offset):
    height = raw.shape[0] // CHUNKS
    count_feat = raw.shape[1]
    span = 256
    return pl.pallas_call(
        bin_kernel,
        grid_spec=pltpu.PrefetchScalarGridSpec(
            num_scalar_prefetch=1,
            grid=(1,),
            in_specs=[
                pl.BlockSpec((height, count_feat), lambda i, c: (part, 0)),
                pl.BlockSpec(memory_space=pltpu.HBM),
                pl.BlockSpec(memory_space=pltpu.HBM),
                pl.BlockSpec((1, count_feat), lambda i, c: (0, 0)),
                pl.BlockSpec((1, count_feat), lambda i, c: (0, 0)),
            ],
            out_specs=pl.BlockSpec((count_feat // span, height, span), lambda i, c: (0, 0, 0)),
            scratch_shapes=[
                pltpu.VMEM((count_feat, 256), jnp.float32),
                pltpu.VMEM((256, 128), jnp.float32),
                pltpu.VMEM((height + 16, count_feat), jnp.bfloat16),
                pltpu.SemaphoreType.DMA((128,)),
            ],
        ),
        out_shape=jax.ShapeDtypeStruct((count_feat // span, height, span), jnp.int16),
        name=f"bin_rows_{part}",
    )(core, raw, mine, other, column, offset)


def local(raw_values, bin_edges, feature_column, bin_offset):
    core = (lax.axis_index("bundle") % 2).astype(jnp.int32).reshape(1)
    mine, other = gather_edges(bin_edges)
    arrived = []
    for part in range(CHUNKS):
        sent = bin_rows(core, raw_values, part, mine, other, feature_column[None], bin_offset[None])
        arrived.append(lax.all_to_all(sent, "bundle", split_axis=0, concat_axis=0, tiled=True))
    codes = jnp.stack(arrived, axis=1)
    return codes.reshape(-1, codes.shape[-1]).astype(jnp.int32)


def solution(mesh):
    in_specs = (P(AXES, None), P(AXES, None), P(), P())
    return jax.shard_map(local, mesh=mesh, in_specs=in_specs, out_specs=P("rows", "bundle"), check_vma=False)
```

time: 403 us -> 149 us (0.37)
  waiting for transfers between devices: 178 us -> 3.92 us
  other arithmetic: 139 us -> 0.59 us
  Pallas kernels: 0 us -> 75.7 us
  local copies, waits for them, and re-layouts: 65.2 us -> 3.41 us
  blocking collectives: 0 us -> 60.6 us
  between operations: 13.5 us -> 0.05 us
    reduce_sum x8 -> x0, other arithmetic: 130 us -> none  [one_block(): jnp.sum(part_rows[:, :, None] > edges[None, :, :], axis=2, dtype=jnp.int32)]
    all_gather x1 -> x0, waiting for transfers between devices: 123 us -> none  [local(): lax.all_gather(bin_edges, ('rows', 'bundle'), axis=0, tiled=True)]
    pallas_call x0 -> x2, Pallas kernels: none -> 75.7 us  [bin_rows(): pl.pallas_call(bin_kernel, grid_spec=pltpu.PrefetchScalarGridSpec(num_sca...]
    all_to_all x0 -> x3, blocking collectives: none -> 60.6 us  [the longest x2 39.7 us: spread(): lax.all_to_all(copies, AXES, split_axis=0, concat_axis=0, axis_index_grou...]
    all_to_all x1, waiting for transfers between devices: 55.1 us -> 0.01 us  [local(): lax.all_to_all(sent, 'bundle', split_axis=0, concat_axis=0, tiled=True)]
    gather x3 -> x0, local copies, waits for them, and re-layouts: 23.3 us -> none  [the longest x1 18.4 us: local(): ordered = jnp.take(raw_values, owner_feature, axis=1)]
    scatter x1 -> x0, local copies, waits for them, and re-layouts: 15.5 us -> none  [local(): owner_feature = jnp.zeros((count_feat,), jnp.int32).at[feature_column].se...]
    gt x8 -> x0, local copies, waits for them, and re-layouts: 8.61 us -> none  [one_block(): part_rows[:, :, None] > edges[None, :, :]]
  transfers between devices with their start and end apart: 2 -> 2, of which waited for: 2 -> 1; matrix products, arithmetic and copies ran while one was open for 13% -> 0% of each run, Pallas kernels for 0% -> 25%
where the time goes in v1:
time: 149 us; the launch traced here: 148 us
  Pallas kernels  75.7 us (51%)
  blocking collectives  60.6 us (41%)
  starting transfers between devices  4.25 us (3%)
  waiting for transfers between devices  3.92 us (3%)
  local copies, waits for them, and re-layouts  3.41 us (2%)
    pallas_call x2, Pallas kernels, bin_rows(): pl.pallas_call(bin_kernel, grid_spec=pltpu.PrefetchScalarGridSpec(num_sca...  75.7 us
    all_to_all x2, blocking collectives, spread(): lax.all_to_all(copies, AXES, split_axis=0, concat_axis=0, axis_index_grou...  39.7 us
    all_to_all x1, blocking collectives, local(): lax.all_to_all(sent, 'bundle', split_axis=0, concat_axis=0, tiled=True)  20.9 us
    ppermute x1, waiting for transfers between devices, gather_edges(): other = lax.ppermute(mine, 'bundle', [(i, i ^ 1) for i in range(16)])  3.92 us
    all_to_all x1, starting transfers between devices, local(): lax.all_to_all(sent, 'bundle', split_axis=0, concat_axis=0, tiled=True)  3.82 us
  transfers between devices with their start and end apart: 2, of which 1 were waited for; matrix products, arithmetic and copies ran while one was open for 0% of the time, Pallas kernels for 25%

profile of v1, /device:TPU:1, one launch (start us, length us, event | category | flops | bytes accessed | tf_op | source)
XLA Modules:
  0.0 148.5 jit_solution(8343047781538573517)
XLA Ops:
  0.0 0.8 pad.4
  0.8 18.2 %all_to_all.20 = f32[16,32,256]{2,1,0:T(8,128)S(1)} all-to-all(f32[16,32,256]{2,1,0:T(8,128)S(1)} %broadcast_in_dim.8), channel_id=1, replica_groups={{0,2,4,6,8,10,12,14,64,66,68,70,72,74,76,78},{16,18,20,22,24,26,28,30,8..., dimensions={0} | all-to-all | bytes 1048576 | tf_op jit(solution)/shard_map/all_to_all | solution.py:29
  19.0 0.2 broadcast_in_dim.9
  19.2 21.5 %all_to_all.21 = f32[4,16,32,256]{3,2,1,0:T(8,128)S(1)} all-to-all(f32[4,16,32,256]{3,2,1,0:T(8,128)S(1)} %broadcast_in_dim.9), channel_id=1, replica_groups={{0,16,32,48},{2,18,34,50},{4,20,36,52},{6,22,38,54},{8,24,40,56},{10,26..., dimensions={0} | all-to-all | bytes 4194304 | tf_op jit(solution)/shard_map/all_to_all | solution.py:29
  40.7 0.0 copy-start
  40.7 0.4 collective-permute-start
  41.2 3.9 %collective-permute-done.other_ref = f32[64,32,256]{2,1,0:T(8,128)} collective-permute-done((f32[64,32,256]{2,1,0:T(8,128)S(1)}, f32[64,32,256]{2,1,0:T(8,128)}, u32[]{:S(2)}, u32[]{:S(2)}) %collective-permute-start) | collective-permute-done | bytes 2097184 | tf_op jit(solution)/shard_map/ppermute | solution.py:37
  45.1 0.0 copy-done
  45.1 37.8 %bin_rows_0.1 = s16[16,128,256]{2,1,0:T(8,128)(2,1)} custom-call(s32[1]{0:T(128)} %bitcast.core_ref, f32[256,4096]{1,0:T(8,128)} %raw_ref.3, f32[64,32,256]{2,1,0:T(8,128)} %bitcast.8, f32[64,32,256]{2,1,0:T(8,128)} %collective-permute-done.other_ref, s32[1,4096]{1,0:T(1,128)} %bitcast.12, s32[1,4096]{1,0:T(1,128)} %bitcast.14), custom_call_target="tpu_custom_call" | custom-call | tf_op jit(solution)/shard_map/bin_rows_0/pallas_call | solution.py:146
  82.9 3.8 %all-to-all-start.2 = ((s16[16,128,256]{2,1,0:T(8,128)(2,1)}), s16[16,128,256]{2,1,0:T(8,128)(2,1)S(1)}, u32[]{:S(2)}, u32[]{:S(2)}) async-start(s16[16,128,256]{2,1,0:T(8,128)(2,1)} %bin_rows_0.1), calls=%async_computation.2 | async-start | bytes 2097152 | tf_op jit(solution)/shard_map/all_to_all | solution.py:177
  86.7 37.8 %bin_rows_1.1 = s16[16,128,256]{2,1,0:T(8,128)(2,1)} custom-call(s32[1]{0:T(128)} %bitcast.core_ref, f32[256,4096]{1,0:T(8,128)} %raw_ref.3, f32[64,32,256]{2,1,0:T(8,128)} %bitcast.9, f32[64,32,256]{2,1,0:T(8,128)} %collective-permute-done.other_ref, s32[1,4096]{1,0:T(1,128)} %bitcast.13, s32[1,4096]{1,0:T(1,128)} %bitcast.15), custom_call_target="tpu_custom_call" | custom-call | tf_op jit(solution)/shard_map/bin_rows_1/pallas_call | solution.py:146
  124.6 0.0 all-to-all-done.2
  124.6 20.9 %all_to_all.22 = s16[16,128,256]{2,1,0:T(8,128)(2,1)S(1)} all-to-all(s16[16,128,256]{2,1,0:T(8,128)(2,1)} %bin_rows_1.1), channel_id=1, replica_groups=mesh['rows'=8,'bundle'=16] {'bundle'}, dimensions={0} | all-to-all | bytes 2097152 | tf_op jit(solution)/shard_map/all_to_all | solution.py:177
  145.5 0.6 add_convert_fusion
  146.1 2.4 %copy.5 = s32[16,2,128,256]{3,2,1,0:T(8,128)} copy(s32[16,2,128,256]{3,2,0,1:T(8,128)S(1)} %add_convert_fusion) | data formatting | bytes 8388608 | tf_op jit(solution)/shard_map/convert_element_type | solution.py:179
  (1 shorter events, 0.0 us)
Async XLA Ops:
  40.7 4.4 %copy-start = (f32[4,16,32,256]{3,2,1,0:T(8,128)}, f32[4,16,32,256]{3,2,1,0:T(8,128)S(1)}, u32[]{:S(2)}) copy-start(f32[4,16,32,256]{3,2,1,0:T(8,128)S(1)} %all_to_all.21) | copy-start | bytes 6291460
  40.7 4.3 %collective-permute-start = (f32[64,32,256]{2,1,0:T(8,128)S(1)}, f32[64,32,256]{2,1,0:T(8,128)}, u32[]{:S(2)}, u32[]{:S(2)}) collective-permute-start(f32[64,32,256]{2,1,0:T(8,128)S(1)} %bitcast.7), channel_id=1, source_target_pairs={{0,1},{1,0},{2,3},{3,2},{4,5},{5,4},{6,7},{7,6},{8,9},{9,8},{10,11... | collective-permute-start | bytes 6291464 | tf_op jit(solution)/shard_map/ppermute | solution.py:37
  82.9 41.7 %all-to-all-start.2 = ((s16[16,128,256]{2,1,0:T(8,128)(2,1)}), s16[16,128,256]{2,1,0:T(8,128)(2,1)S(1)}, u32[]{:S(2)}, u32[]{:S(2)}) async-start(s16[16,128,256]{2,1,0:T(8,128)(2,1)} %bin_rows_0.1), calls=%async_computation.2 | async-start | bytes 2097152 | tf_op jit(solution)/shard_map/all_to_all | solution.py:177
